TPU v7x, 32 devices: a whole 2x2x4 slice. The times are simulated.
32 devices in a mesh: scen: 8 (over z, y), gen: 4 (over x, core).
Axes of the slice: x: 2, y: 2, z: 4, core: 2. Of those that a mesh axis runs over, the one named last changes fastest.
Arguments:
- zone_load: float32 [128, 16, 256], P('scen'), may hold values from 0.3 to 1
- linear_cost: float32 [16, 20480], P(None, 'gen'), may hold values from -4 to 4
- cost_diag: float32 [20480], P('gen'), may hold values from 0.5 to 2
- capacity: float32 [20480], P('gen'), may hold values from 0.5 to 2
- cost_tiles: bfloat16 [80, 256, 256], P('gen'), may hold values from -0.375 to 0.375
- coupling_tiles: bfloat16 [8, 80, 256, 256], P('scen', 'gen'), may hold values from -0.375 to 0.375
- block_map: int32 [8, 80], P('scen', 'gen'), may hold values 0 or 1
- zone_index: int32 [20480], P('gen'), may hold values from 0 to 255
- step_numer: int32 [5], replicated, may hold values from 1 to 4
- step_denom: int32 [5], replicated, may hold values from 5 to 8
Outputs:
- dispatch: float32 [128, 16, 20480], P('scen', None, 'gen')
- prices: float32 [128, 16, 256], P('scen')
- plan: float32 [16, 20480], P(None, 'gen')
All inputs are finite; a program needn't handle non-finite values. No bound on the sum of `block_map` on one device may be relied on, other than what follows from the above.
Results may differ from a plain program's by a relative error of at most 0.0003.
Values sent between devices are 32-bit elements; how exact they have to be, the bound alone decides.
No kernel may reach another device: no remote copies, remote signals or barrier semaphores. Data moves between devices by JAX's collectives and lax.ppermute only.
A program may use at most 128 MiB of HBM per device.

v0:
```python
import jax
import jax.numpy as jnp
from jax import lax
from jax.sharding import PartitionSpec as P

G = 20480
ITERS = 5
penalty = 2.0
centering = 0.5
epsilon = 1e-06


def local(
    zone_load,
    linear_cost,
    cost_diag,
    capacity,
    cost_tiles,
    coupling_tiles,
    block_map,
    zone_index,
    step_numer,
    step_denom,
):
    local_scen = zone_load.shape[0]
    periods = linear_cost.shape[0]
    zone_count = zone_load.shape[2]
    local_gen = capacity.shape[0]
    local_blocks = cost_tiles.shape[0]
    tile_width = cost_tiles.shape[2]
    gen_devices = lax.axis_size("gen")
    total_scen = local_scen * lax.axis_size("scen")
    row_count = local_scen * periods
    entries = float(total_scen * periods * G)
    coupling = coupling_tiles[0]
    block_mask = block_map[0].astype(jnp.float32)
    onehot = (zone_index[:, None] == jnp.arange(zone_count, dtype=jnp.int32)[None, :]).astype(
        jnp.float32
    )
    scen_ids = lax.axis_index("scen") * local_scen + jnp.arange(local_scen, dtype=jnp.int32)
    levels = 0.2 + 0.6 * (scen_ids.astype(jnp.float32) + 0.5) / total_scen
    dispatch = jnp.broadcast_to(levels[:, None, None] * capacity, (local_scen, periods, local_gen))
    low_dual = jnp.ones((local_scen, periods, local_gen), jnp.float32)
    high_dual = jnp.ones((local_scen, periods, local_gen), jnp.float32)
    prices = jnp.zeros((local_scen, periods, zone_count), jnp.float32)
    lowest = 0.02 * capacity
    highest = 0.98 * capacity
    plan = jnp.zeros((periods, local_gen), jnp.float32)
    for iteration in range(ITERS):
        step_size = step_numer[iteration].astype(jnp.float32) / step_denom[iteration].astype(
            jnp.float32
        )
        column_sums = lax.psum(jnp.sum(dispatch, axis=0), "scen")
        plan = column_sums / total_scen
        partial_value = jnp.dot(
            dispatch.reshape(row_count, local_gen),
            onehot,
            precision=lax.Precision.HIGHEST,
            preferred_element_type=jnp.float32,
        )
        totals = lax.psum(partial_value, "gen")
        imbalance = totals.reshape(local_scen, periods, zone_count) * (zone_count / G) - zone_load
        primal_local = jnp.sum(imbalance * imbalance) / gen_devices
        rounded = dispatch.astype(jnp.bfloat16).reshape(row_count, local_blocks, tile_width)
        cross_part = jnp.einsum(
            "rki,kij->rkj", rounded, coupling, preferred_element_type=jnp.float32
        )
        own_part = jnp.einsum(
            "rki,kij->rkj", rounded, cost_tiles, preferred_element_type=jnp.float32
        )
        products = (own_part + cross_part * block_mask[None, :, None]).reshape(
            local_scen, periods, local_gen
        )
        price_terms = jnp.dot(
            prices.reshape(row_count, zone_count),
            onehot.T,
            precision=lax.Precision.HIGHEST,
            preferred_element_type=jnp.float32,
        )
        residual = (
            cost_diag * dispatch
            + products
            + linear_cost
            + penalty * (dispatch - plan)
            + price_terms.reshape(local_scen, periods, local_gen)
            - low_dual
            + high_dual
        )
        gap_local = jnp.sum(dispatch * low_dual + (capacity - dispatch) * high_dual)
        dual_local = jnp.sum(residual * residual)
        stacked = jnp.stack([gap_local, dual_local, primal_local])
        summed = lax.psum(stacked, ("scen", "gen"))
        gap_sum = summed[0]
        dual_sq = summed[1]
        primal_sq = summed[2]
        target = centering * gap_sum / (2.0 * entries)
        dual_rms = jnp.sqrt(dual_sq / entries + epsilon)
        primal_rms = jnp.sqrt(primal_sq / float(total_scen * periods * zone_count) + epsilon)
        scaling = cost_diag + penalty + low_dual / dispatch + high_dual / (capacity - dispatch)
        updated = jnp.clip(
            dispatch - step_size * residual / (scaling * (1.0 + dual_rms)), lowest, highest
        )
        low_dual = low_dual + step_size * (target / updated - low_dual)
        high_dual = high_dual + step_size * (target / (capacity - updated) - high_dual)
        prices = prices + step_size * imbalance / (1.0 + primal_rms)
        dispatch = updated
    return (dispatch, prices, plan)


def solution(mesh):
    placed = (
        P("scen", None, None),
        P(None, "gen"),
        P("gen"),
        P("gen"),
        P("gen", None, None),
        P("scen", "gen", None, None),
        P("scen", "gen"),
        P("gen"),
        P(),
        P(),
    )
    return jax.shard_map(
        local,
        mesh=mesh,
        in_specs=placed,
        out_specs=(P("scen", None, "gen"), P("scen", None, None), P(None, "gen")),
        check_vma=False,
    )
```

profile of v0, /device:TPU:0, one launch (start us, length us, event | category | flops | bytes accessed | tf_op | source)
XLA Modules:
  0.0 921.3 jit_solution(15415761440046506945)
XLA Ops:
  36.5 5.7 copy.38
  42.3 7.0 reshape.258
  52.3 71.3 %all-reduce.11.cloned.1.call-done = f32[16,5120]{1,0:T(8,128)} async-done(((f32[16,5120]{1,0:T(8,128)}), f32[16,5120]{1,0:T(8,128)}) %all-reduce.11.cloned.1.call-update) | async-done | bytes 327696 | tf_op jit(solution)/shard_map/psum | solution.py:53
  124.6 9.1 multiply_reduce_fusion.4
  135.1 40.0 %psum.107 = f32[3]{0:T(128)S(1)} all-reduce(f32[3]{0:T(128)S(1)} %pad_maximum_fusion), channel_id=1, replica_groups=mesh['scen'=8,'gen'=4] {'scen','gen'}, use_global_device_ids=true, to_apply=%region_6.0 | all-reduce | flops 3 | bytes 24 | tf_op jit(solution)/shard_map/psum | solution.py:92
  177.1 6.8 add_reduce_fusion.3
  201.9 5.7 copy.41
  207.7 7.0 reshape.262
  214.9 8.1 all-reduce.17.cloned.1.call-done
  225.3 72.3 %all-reduce.15.cloned.1.call-done = f32[16,5120]{1,0:T(8,128)} async-done(((f32[16,5120]{1,0:T(8,128)}), f32[16,5120]{1,0:T(8,128)}) %all-reduce.15.cloned.1.call-update) | async-done | bytes 327696 | tf_op jit(solution)/shard_map/psum | solution.py:53
  298.7 11.3 %multiply_reduce_fusion.3 = (f32[]{:T(128)}, f32[16,16,5120]{2,1,0:T(8,128)}) fusion(f32[16,16,5120]{2,1,0:T(8,128)} %copy-done.1, f32[5120]{0:T(1024)S(1)} %copy-done.17, f32[]{:T(128)} %bitcast.14, f32[]{:T(128)} %bitcast, s32[5120]{0:T(1024)S(1)} %copy-done.23, f32[]{:T(128)} %bitcast.13, f32[16,16,256]{2,1,0:T(8,128)S(1)} %bitcast.123, ...), kind=kOutput, calls=%fused_computation.38 | convolution fusion | flops 4054253568 | bytes 16969744 | tf_op jit(solution)/shard_map/dot_general | solution.py:74
  311.5 39.5 %psum.110 = f32[3]{0:T(128)S(1)} all-reduce(f32[3]{0:T(128)S(1)} %pad_maximum_fusion.1), channel_id=1, replica_groups=mesh['scen'=8,'gen'=4] {'scen','gen'}, use_global_device_ids=true, to_apply=%region_13.14 | all-reduce | flops 3 | bytes 24 | tf_op jit(solution)/shard_map/psum | solution.py:92
  353.0 9.8 %add_reduce_fusion.2 = (f32[]{:T(128)}, f32[16,5120]{1,0:T(8,128)}, f32[16,16,5120]{2,1,0:T(8,128)S(1)}) fusion(f32[5120]{0:T(1024)S(1)} %copy-done.17, f32[]{:T(128)} %bitcast.24, f32[]{:T(128)} %bitcast.11, f32[16,16,5120]{2,1,0:T(8,128)} %copy-done.1, f32[]{:T(128)} %bitcast.14, f32[]{:T(128)} %bitcast, f32[]{:T(128)} %bitcast.20, ...), kind=kLoop, calls=%fused_computation.33 | loop fusion | flops 43171840 | bytes 16138264 | tf_op jit(solution)/shard_map/reduce_sum | solution.py:89
  381.0 5.7 copy.44
  386.8 7.0 reshape.265
  393.9 8.0 all-reduce.21.cloned.1.call-done
  405.2 71.9 %all-reduce.19.cloned.1.call-done = f32[16,5120]{1,0:T(8,128)} async-done(((f32[16,5120]{1,0:T(8,128)}), f32[16,5120]{1,0:T(8,128)}) %all-reduce.19.cloned.1.call-update) | async-done | bytes 327696 | tf_op jit(solution)/shard_map/psum | solution.py:53
  478.1 13.2 %multiply_reduce_fusion.2 = (f32[]{:T(128)}, f32[16,16,5120]{2,1,0:T(8,128)}) fusion(f32[16,16,5120]{2,1,0:T(8,128)} %copy-done.4, f32[16,16,5120]{2,1,0:T(8,128)} %copy-done.1, f32[5120]{0:T(1024)S(1)} %copy-done.17, f32[]{:T(128)} %bitcast.24, f32[]{:T(128)} %bitcast.11, f32[]{:T(128)} %bitcast.14, f32[]{:T(128)} %bitcast, ...), kind=kOutput, calls=%fused_computation.32 | convolution fusion | flops 4065853440 | bytes 21950484 | tf_op jit(solution)/shard_map/dot_general | solution.py:74
  492.7 39.8 %psum.113 = f32[3]{0:T(128)S(1)} all-reduce(f32[3]{0:T(128)S(1)} %pad_maximum_fusion.2), channel_id=1, replica_groups=mesh['scen'=8,'gen'=4] {'scen','gen'}, use_global_device_ids=true, to_apply=%region_20.21 | all-reduce | flops 3 | bytes 24 | tf_op jit(solution)/shard_map/psum | solution.py:92
  534.5 14.1 %add_reduce_fusion.1 = (f32[]{:T(128)}, f32[16,5120]{1,0:T(8,128)}, f32[16,16,5120]{2,1,0:T(8,128)}, f32[16,16,5120]{2,1,0:T(8,128)}, f32[16,16,5120]{2,1,0:T(8,128)S(1)}) fusion(f32[5120]{0:T(1024)S(1)} %copy-done.17, f32[]{:T(128)} %bitcast.34, f32[]{:T(128)} %bitcast.21, f32[16,16,5120]{2,1,0:T(8,128)} %copy-done.4, f32[]{:T(128)} %bitcast.24, ...), kind=kLoop, calls=%fused_computation.27 | loop fusion | flops 54968320 | bytes 31866912 | tf_op jit(solution)/shard_map/reduce_sum | solution.py:89
  572.9 7.0 reshape.268
  580.0 7.8 all-reduce.25.cloned.1.call-done
  590.1 73.0 %all-reduce.23.cloned.1.call-done = f32[16,5120]{1,0:T(8,128)} async-done(((f32[16,5120]{1,0:T(8,128)}), f32[16,5120]{1,0:T(8,128)}) %all-reduce.23.cloned.1.call-update) | async-done | bytes 327696 | tf_op jit(solution)/shard_map/psum | solution.py:53
  664.2 12.4 %multiply_reduce_fusion.1 = (f32[]{:T(128)}, f32[16,16,5120]{2,1,0:T(8,128)}) fusion(f32[16,16,5120]{2,1,0:T(8,128)} %get-tuple-element.13, f32[16,16,5120]{2,1,0:T(8,128)} %get-tuple-element.12, s32[5120]{0:T(1024)S(1)} %copy-done.23, f32[16,16,256]{2,1,0:T(8,128)S(1)} %get-tuple-element.19, f32[]{:T(128)} %bitcast.33, f32[]{:T(128)} %bitcast.21, ...), kind=kOutput, calls=%fused_computation.26 | convolution fusion | flops 4042588160 | bytes 27697164 | tf_op jit(solution)/shard_map/dot_general | solution.py:74
  677.9 39.7 %psum.116 = f32[3]{0:T(128)S(1)} all-reduce(f32[3]{0:T(128)S(1)} %pad_maximum_fusion.3), channel_id=1, replica_groups=mesh['scen'=8,'gen'=4] {'scen','gen'}, use_global_device_ids=true, to_apply=%region_27.28 | all-reduce | flops 3 | bytes 24 | tf_op jit(solution)/shard_map/psum | solution.py:92
  719.6 10.6 %add_reduce_fusion = (f32[]{:T(128)}, f32[16,5120]{1,0:T(8,128)}, f32[16,16,5120]{2,1,0:T(8,128)S(1)}) fusion(f32[5120]{0:T(1024)S(1)} %copy-done.17, f32[16,16,5120]{2,1,0:T(8,128)} %get-tuple-element.12, f32[]{:T(128)} %bitcast.44, f32[]{:T(128)} %bitcast.31, f32[16,16,5120]{2,1,0:T(8,128)} %get-tuple-element.13, f32[16,16,5120]{2,1,0:T(8,128)} %copy-done.2, ...), kind=kLoop, calls=%fused_computation.21 | loop fusion | flops 32686080 | bytes 26624016 | tf_op jit(solution)/shard_map/reduce_sum | solution.py:89
  754.2 7.0 reshape.271
  761.2 8.1 all-reduce.29.cloned.1.call-done
  773.5 71.1 %all-reduce.27.cloned.1.call-done = f32[16,5120]{1,0:T(8,128)} async-done(((f32[16,5120]{1,0:T(8,128)}), f32[16,5120]{1,0:T(8,128)}) %all-reduce.27.cloned.1.call-update) | async-done | bytes 327696 | tf_op jit(solution)/shard_map/psum | solution.py:53
  845.5 14.3 %multiply_reduce_fusion = (f32[]{:T(128)}, f32[16,16,5120]{2,1,0:T(8,128)}) fusion(f32[16,16,5120]{2,1,0:T(8,128)} %get-tuple-element.13, f32[16,16,5120]{2,1,0:T(8,128)} %copy-done.3, f32[5120]{0:T(1024)S(1)} %copy-done.17, f32[16,16,5120]{2,1,0:T(8,128)} %get-tuple-element.12, f32[]{:T(128)} %bitcast.44, f32[]{:T(128)} %bitcast.31, ...), kind=kOutput, calls=%fused_computation.20 | convolution fusion | flops 4054056960 | bytes 27193356 | tf_op jit(solution)/shard_map/dot_general | solution.py:74
  861.2 39.5 %psum.119 = f32[3]{0:T(128)S(1)} all-reduce(f32[3]{0:T(128)S(1)} %pad_maximum_fusion.4), channel_id=1, replica_groups=mesh['scen'=8,'gen'=4] {'scen','gen'}, use_global_device_ids=true, to_apply=%region_34.35 | all-reduce | flops 3 | bytes 24 | tf_op jit(solution)/shard_map/psum | solution.py:92
  902.7 10.7 %maximum_minimum_fusion = f32[16,16,5120]{2,1,0:T(8,128)} fusion(f32[16,16,5120]{2,1,0:T(8,128)} %copy-done.3, f32[16,16,5120]{2,1,0:T(8,128)} %get-tuple-element.59, f32[]{:T(128)} %bitcast.50, f32[]{:T(128)} %bitcast.41, f32[5120]{0:T(1024)S(1)} %copy-done.17, f32[5120]{0:T(1024)S(1)} %broadcast_add_fusion, f32[5120]{0:T(1024)S(1)} %get-tuple-element.25, ...), kind=kLoop, calls=%fused_computation.19 | loop fusion | flops 24903680 | bytes 26296336 | tf_op jit(solution)/shard_map/jit(clip)/min | solution.py:100
  (143 shorter events, 132.3 us)
Async XLA Ops:
  7.2 24.8 %copy-start = (bf16[20,256,256]{2,1,0:T(8,128)(2,1)S(1)}, bf16[20,256,256]{2,1,0:T(8,128)(2,1)}, u32[]{:S(2)}) copy-start(bf16[20,256,256]{2,1,0:T(8,128)(2,1)} %param.14) | copy-start | bytes 7864324
  7.2 42.1 %all-reduce.13.cloned.1.call-start = ((), (), s32[]{:S(2)}) async-start(), calls=%async_computation.1 | async-start | bytes 524288 | tf_op jit(solution)/shard_map/psum | solution.py:61
  9.0 4.7 copy-start.17
  9.0 7.9 copy-start.28
  9.0 7.9 copy-start.26
  9.0 11.8 %copy-start.27 = (s32[5]{0:T(128)S(1)}, s32[5]{0:T(128)}, u32[]{:S(2)}) copy-start(s32[5]{0:T(128)} %param.19) | copy-start | bytes 64
  9.0 15.6 %copy-start.25 = (f32[5120]{0:T(1024)S(1)}, f32[5120]{0:T(1024)}, u32[]{:S(2)}) copy-start(f32[5120]{0:T(1024)} %param.12) | copy-start | bytes 61444
  13.6 110.0 %all-reduce.11.cloned.1.call-start = ((), (), s32[]{:S(2)}) async-start(), calls=%async_computation | async-start | bytes 655360 | tf_op jit(solution)/shard_map/psum | solution.py:53
  14.6 208.5 %all-reduce.17.cloned.1.call-start = ((), (), s32[]{:S(2)}) async-start(), calls=%async_computation.3 | async-start | bytes 524288 | tf_op jit(solution)/shard_map/psum | solution.py:61
  31.9 3.6 copy-start.11
  42.3 8.7 copy-start.15
  183.8 3.1 copy-start.1
  191.0 106.7 %all-reduce.15.cloned.1.call-start = ((), (), s32[]{:S(2)}) async-start(), calls=%async_computation.2 | async-start | bytes 655360 | tf_op jit(solution)/shard_map/psum | solution.py:53
  196.6 3.6 copy-start.12
  207.7 91.0 %copy-start.21 = (f32[256,256]{1,0:T(8,128)S(1)}, f32[256,256]{1,0:T(8,128)}, u32[]{:S(2)}) copy-start(f32[256,256]{1,0:T(8,128)} %copy-done.20) | copy-start | bytes 786436
  214.7 187.2 %all-reduce.21.cloned.1.call-start = ((), (), s32[]{:S(2)}) async-start(), calls=%async_computation.5 | async-start | bytes 524288 | tf_op jit(solution)/shard_map/psum | solution.py:61
  362.8 3.1 copy-start.4
  369.8 107.2 %all-reduce.19.cloned.1.call-start = ((), (), s32[]{:S(2)}) async-start(), calls=%async_computation.4 | async-start | bytes 655360 | tf_op jit(solution)/shard_map/psum | solution.py:53
  375.7 3.6 copy-start.13
  386.8 16.1 %copy-start.18 = (f32[256,256]{1,0:T(8,128)S(1)}, f32[256,256]{1,0:T(8,128)}, u32[]{:S(2)}) copy-start(f32[256,256]{1,0:T(8,128)} %all-reduce.13.cloned.1.call-done) | copy-start | bytes 786436
  393.8 194.0 %all-reduce.25.cloned.1.call-start = ((), (), s32[]{:S(2)}) async-start(), calls=%async_computation.7 | async-start | bytes 524288 | tf_op jit(solution)/shard_map/psum | solution.py:61
  548.7 3.1 copy-start.2
  555.7 107.4 %all-reduce.23.cloned.1.call-start = ((), (), s32[]{:S(2)}) async-start(), calls=%async_computation.6 | async-start | bytes 655360 | tf_op jit(solution)/shard_map/psum | solution.py:53
  561.8 3.6 copy-start.14
  572.9 91.2 %copy-start.16 = (f32[256,256]{1,0:T(8,128)S(1)}, f32[256,256]{1,0:T(8,128)}, u32[]{:S(2)}) copy-start(f32[256,256]{1,0:T(8,128)} %all-reduce.21.cloned.1.call-done) | copy-start | bytes 786436
  580.0 189.3 %all-reduce.29.cloned.1.call-start = ((), (), s32[]{:S(2)}) async-start(), calls=%async_computation.9 | async-start | bytes 524288 | tf_op jit(solution)/shard_map/psum | solution.py:61
  730.2 3.1 copy-start.3
  737.2 107.3 %all-reduce.27.cloned.1.call-start = ((), (), s32[]{:S(2)}) async-start(), calls=%async_computation.8 | async-start | bytes 655360 | tf_op jit(solution)/shard_map/psum | solution.py:53
  743.1 3.6 copy-start.10
  845.5 14.3 %copy-start.24 = (f32[16,5120]{1,0:T(8,128)}, f32[16,5120]{1,0:T(8,128)S(1)}, u32[]{:S(2)}) copy-start(f32[16,5120]{1,0:T(8,128)S(1)} %broadcast_multiply_fusion) | copy-start | bytes 983044
  902.7 10.7 %copy-start.19 = (f32[256,256]{1,0:T(8,128)S(1)}, f32[256,256]{1,0:T(8,128)}, u32[]{:S(2)}) copy-start(f32[256,256]{1,0:T(8,128)} %all-reduce.29.cloned.1.call-done) | copy-start | bytes 786436
  902.7 10.7 %copy-start.22 = (f32[16,16,256]{2,1,0:T(8,128)S(1)}, f32[16,16,256]{2,1,0:T(8,128)}, u32[]{:S(2)}) copy-start(f32[16,16,256]{2,1,0:T(8,128)} %get-tuple-element.18) | copy-start | bytes 786436
  (7 other events, 17.7 us)
Sparse Core Ops, SparseCore 0:
  13.7 35.0 all-reduce.12
  52.1 71.3 all-reduce.10
  191.1 31.9 all-reduce.16
  226.3 71.3 all-reduce.14
  370.0 31.8 all-reduce.20
  405.7 71.3 all-reduce.18
  555.8 31.9 all-reduce.24
  591.7 71.3 all-reduce.22
  737.4 31.9 all-reduce.28
  773.1 71.3 all-reduce.26
where the time goes:
time: 927 us; the launch traced here: 921 us
  waiting for transfers between devices  392 us (42%)
  blocking collectives  199 us (21%)
  local copies, waits for them, and re-layouts  108 us (12%)
  matrix products  99.4 us (11%)
  other arithmetic  87.8 us (9%)
  between operations  34.2 us (4%)
    psum x5, waiting for transfers between devices, local(): column_sums = lax.psum(jnp.sum(dispatch, axis=0), 'scen')  360 us
    psum x5, blocking collectives, local(): summed = lax.psum(stacked, ('scen', 'gen'))  199 us
    dot_general x5, matrix products, local(): jnp.dot(prices.reshape(row_count, zone_count), onehot.T, precision=lax.Pr...  60.4 us
    reduce_sum x5, other arithmetic, local(): gap_local = jnp.sum(dispatch * low_dual + (capacity - dispatch) * high_dual)  43.2 us
    reshape x5, local copies, waits for them, and re-layouts, local(): (own_part + cross_part * block_mask[None, :, None]).reshape(local_scen, p...  35 us
    psum x5, waiting for transfers between devices, local(): totals = lax.psum(partial_value, 'gen')  32 us
    add x5, local copies, waits for them, and re-layouts, local(): own_part + cross_part * block_mask[None, :, None]  28.7 us
    reshape x5, local copies, waits for them, and re-layouts, local(): dispatch.astype(jnp.bfloat16).reshape(row_count, local_blocks, tile_width)  27.8 us
  transfers between devices with their start and end apart: 10, of which 9 were waited for; matrix products, arithmetic and copies ran while one was open for 14% of the time, Pallas kernels for 0%

commit v1 on v0

--- a/solution.py
+++ b/solution.py
@@ -50,7 +50,7 @@
         step_size = step_numer[iteration].astype(jnp.float32) / step_denom[iteration].astype(
             jnp.float32
         )
-        column_sums = lax.psum(jnp.sum(dispatch, axis=0), "scen")
+        column_sums = jnp.sum(lax.all_gather(jnp.sum(dispatch, axis=0), "scen"), axis=0)
         plan = column_sums / total_scen
         partial_value = jnp.dot(
             dispatch.reshape(row_count, local_gen),

time: 927 us -> 817 us (0.88)
  waiting for transfers between devices: 392 us -> 229 us
  blocking collectives: 199 us -> 231 us
  other arithmetic: 87.8 us -> 103 us
    psum x5 -> x0, waiting for transfers between devices: 360 us -> none  [local(): column_sums = lax.psum(jnp.sum(dispatch, axis=0), 'scen')]
    all_gather x0 -> x4, waiting for transfers between devices: none -> 216 us  [local(): lax.all_gather(jnp.sum(dispatch, axis=0), 'scen')]
    all_gather x0 -> x1, blocking collectives: none -> 32.7 us  [local(): lax.all_gather(jnp.sum(dispatch, axis=0), 'scen')]
    psum x5, waiting for transfers between devices: 32 us -> 10.6 us  [local(): totals = lax.psum(partial_value, 'gen')]
  transfers between devices with their start and end apart: 10 -> 9, of which waited for: 9 -> 8; matrix products, arithmetic and copies ran while one was open for 14% -> 19% of each run, Pallas kernels for 0% -> 0%
where the time goes in v1:
time: 817 us; the launch traced here: 810 us
  blocking collectives  231 us (28%)
  waiting for transfers between devices  229 us (28%)
  local copies, waits for them, and re-layouts  113 us (14%)
  other arithmetic  103 us (13%)
  matrix products  99.4 us (12%)
  between operations  33.3 us (4%)
    all_gather x4, waiting for transfers between devices, local(): lax.all_gather(jnp.sum(dispatch, axis=0), 'scen')  216 us
    psum x5, blocking collectives, local(): summed = lax.psum(stacked, ('scen', 'gen'))  198 us
    dot_general x5, matrix products, local(): jnp.dot(prices.reshape(row_count, zone_count), onehot.T, precision=lax.Pr...  60.4 us
    reduce_sum x5, other arithmetic, local(): gap_local = jnp.sum(dispatch * low_dual + (capacity - dispatch) * high_dual)  43.2 us
    reshape x5, local copies, waits for them, and re-layouts, local(): (own_part + cross_part * block_mask[None, :, None]).reshape(local_scen, p...  34.9 us
    all_gather x1, blocking collectives, local(): lax.all_gather(jnp.sum(dispatch, axis=0), 'scen')  32.7 us
    add x5, local copies, waits for them, and re-layouts, local(): own_part + cross_part * block_mask[None, :, None]  28.7 us
    reshape x5, local copies, waits for them, and re-layouts, local(): dispatch.astype(jnp.bfloat16).reshape(row_count, local_blocks, tile_width)  27.8 us
  transfers between devices with their start and end apart: 9, of which 8 were waited for; matrix products, arithmetic and copies ran while one was open for 19% of the time, Pallas kernels for 0%

profile of v1, /device:TPU:0, one launch (start us, length us, event | category | flops | bytes accessed | tf_op | source)
XLA Modules:
  0.0 810.1 jit_solution(12163853243281500481)
XLA Ops:
  18.3 32.7 %all-gather = f32[40960]{0:T(1024)S(1)} all-gather(f32[5120]{0:T(1024)S(1)} %multiply_reduce_fusion.5), channel_id=3, replica_groups=mesh['scen'=8,'gen'=4] {'scen'}, dimensions={0}, use_global_device_ids=true | all-gather | bytes 184320 | tf_op jit(solution)/shard_map/all_gather | solution.py:53
  64.7 5.7 copy.53
  70.5 6.9 reshape.268
  77.4 9.1 %multiply_reduce_fusion.4 = (f32[]{:T(128)}, f32[16,16,5120]{2,1,0:T(8,128)}) fusion(s32[5120]{0:T(1024)S(1)} %copy-done.22, f32[16,5120]{1,0:T(8,128)} %broadcast_multiply_fusion.4, f32[16,5120]{1,0:T(8,128)} %param.11, f32[16,16,5120]{2,1,0:T(8,128)} %reshape.268, f32[16,5120]{1,0:T(8,128)S(1)} %get-tuple-element.22, f32[5120]{0:T(1024)S(1)} %copy-done.24), kind=kOutput, calls=%fused_computation.44 | convolution fusion | flops 4039639040 | bytes 11509764 | tf_op jit(solution)/shard_map/dot_general | solution.py:74
  90.8 40.1 %psum.71 = f32[3]{0:T(128)S(1)} all-reduce(f32[3]{0:T(128)S(1)} %pad_maximum_fusion), channel_id=1, replica_groups=mesh['scen'=8,'gen'=4] {'scen','gen'}, use_global_device_ids=true, to_apply=%region_6.0 | all-reduce | flops 3 | bytes 24 | tf_op jit(solution)/shard_map/psum | solution.py:92
  132.9 6.8 add_reduce_fusion.3
  163.4 5.7 copy.56
  169.1 7.0 reshape.272
  181.2 54.3 %all-gather.10.cloned.1.call-done = f32[128,5120]{1,0:T(8,128)} async-done(((f32[16,5120]{1,0:T(8,128)}), f32[128,5120]{1,0:T(8,128)}) %all-gather.10.cloned.1.call-update) | async-done | bytes 2621456 | tf_op jit(solution)/shard_map/all_gather | solution.py:53
  237.4 11.4 %multiply_reduce_fusion.3 = (f32[]{:T(128)}, f32[16,16,5120]{2,1,0:T(8,128)}) fusion(f32[16,16,5120]{2,1,0:T(8,128)} %copy-done.1, f32[5120]{0:T(1024)S(1)} %copy-done.17, f32[]{:T(128)} %bitcast.15, f32[]{:T(128)} %bitcast, s32[5120]{0:T(1024)S(1)} %copy-done.22, f32[]{:T(128)} %bitcast.14, f32[16,16,256]{2,1,0:T(8,128)} %bitcast.131, ...), kind=kOutput, calls=%fused_computation.38 | convolution fusion | flops 4054253568 | bytes 16969744 | tf_op jit(solution)/shard_map/dot_general | solution.py:74
  250.1 39.4 %psum.73 = f32[3]{0:T(128)S(1)} all-reduce(f32[3]{0:T(128)S(1)} %pad_maximum_fusion.1), channel_id=1, replica_groups=mesh['scen'=8,'gen'=4] {'scen','gen'}, use_global_device_ids=true, to_apply=%region_13.14 | all-reduce | flops 3 | bytes 24 | tf_op jit(solution)/shard_map/psum | solution.py:92
  291.6 9.8 %add_reduce_fusion.2 = (f32[]{:T(128)}, f32[16,5120]{1,0:T(8,128)}, f32[16,16,5120]{2,1,0:T(8,128)S(1)}) fusion(f32[5120]{0:T(1024)S(1)} %copy-done.17, f32[]{:T(128)} %bitcast.26, f32[]{:T(128)} %bitcast.11, f32[16,16,5120]{2,1,0:T(8,128)} %copy-done.1, f32[]{:T(128)} %bitcast.15, f32[]{:T(128)} %bitcast, f32[]{:T(128)} %bitcast.21, ...), kind=kLoop, calls=%fused_computation.33 | loop fusion | flops 43171840 | bytes 16138264 | tf_op jit(solution)/shard_map/reduce_sum | solution.py:89
  314.9 5.6 reshape.274
  325.1 5.7 copy.59
  330.9 7.0 reshape.275
  343.7 53.7 %all-gather.12.cloned.1.call-done = f32[128,5120]{1,0:T(8,128)} async-done(((f32[16,5120]{1,0:T(8,128)}), f32[128,5120]{1,0:T(8,128)}) %all-gather.12.cloned.1.call-update) | async-done | bytes 2621456 | tf_op jit(solution)/shard_map/all_gather | solution.py:53
  401.0 13.2 %multiply_reduce_fusion.2 = (f32[]{:T(128)}, f32[16,16,5120]{2,1,0:T(8,128)}) fusion(f32[16,16,5120]{2,1,0:T(8,128)} %copy-done.4, f32[16,16,5120]{2,1,0:T(8,128)} %copy-done.1, f32[5120]{0:T(1024)S(1)} %copy-done.17, f32[]{:T(128)} %bitcast.26, f32[]{:T(128)} %bitcast.11, f32[]{:T(128)} %bitcast.15, f32[]{:T(128)} %bitcast, ...), kind=kOutput, calls=%fused_computation.32 | convolution fusion | flops 4065853440 | bytes 21950484 | tf_op jit(solution)/shard_map/dot_general | solution.py:74
  415.6 39.7 %psum.75 = f32[3]{0:T(128)S(1)} all-reduce(f32[3]{0:T(128)S(1)} %pad_maximum_fusion.2), channel_id=1, replica_groups=mesh['scen'=8,'gen'=4] {'scen','gen'}, use_global_device_ids=true, to_apply=%region_20.21 | all-reduce | flops 3 | bytes 24 | tf_op jit(solution)/shard_map/psum | solution.py:92
  457.2 14.1 %add_reduce_fusion.1 = (f32[]{:T(128)}, f32[16,5120]{1,0:T(8,128)}, f32[16,16,5120]{2,1,0:T(8,128)}, f32[16,16,5120]{2,1,0:T(8,128)}, f32[16,16,5120]{2,1,0:T(8,128)S(1)}) fusion(f32[5120]{0:T(1024)S(1)} %copy-done.17, f32[]{:T(128)} %bitcast.37, f32[]{:T(128)} %bitcast.22, f32[16,16,5120]{2,1,0:T(8,128)} %copy-done.4, f32[]{:T(128)} %bitcast.26, ...), kind=kLoop, calls=%fused_computation.27 | loop fusion | flops 54968320 | bytes 31866912 | tf_op jit(solution)/shard_map/reduce_sum | solution.py:89
  495.0 5.7 copy.62
  500.7 7.0 reshape.278
  512.6 54.9 %all-gather.14.cloned.1.call-done = f32[128,5120]{1,0:T(8,128)} async-done(((f32[16,5120]{1,0:T(8,128)}), f32[128,5120]{1,0:T(8,128)}) %all-gather.14.cloned.1.call-update) | async-done | bytes 2621456 | tf_op jit(solution)/shard_map/all_gather | solution.py:53
  571.1 12.4 %multiply_reduce_fusion.1 = (f32[]{:T(128)}, f32[16,16,5120]{2,1,0:T(8,128)}) fusion(f32[16,16,5120]{2,1,0:T(8,128)} %get-tuple-element.13, f32[16,16,5120]{2,1,0:T(8,128)} %get-tuple-element.12, s32[5120]{0:T(1024)S(1)} %copy-done.22, f32[16,16,256]{2,1,0:T(8,128)S(1)} %get-tuple-element.19, f32[]{:T(128)} %bitcast.36, f32[]{:T(128)} %bitcast.22, ...), kind=kOutput, calls=%fused_computation.26 | convolution fusion | flops 4042588160 | bytes 27697164 | tf_op jit(solution)/shard_map/dot_general | solution.py:74
  585.0 39.4 %psum.77 = f32[3]{0:T(128)S(1)} all-reduce(f32[3]{0:T(128)S(1)} %pad_maximum_fusion.3), channel_id=1, replica_groups=mesh['scen'=8,'gen'=4] {'scen','gen'}, use_global_device_ids=true, to_apply=%region_27.28 | all-reduce | flops 3 | bytes 24 | tf_op jit(solution)/shard_map/psum | solution.py:92
  626.4 10.6 %add_reduce_fusion = (f32[]{:T(128)}, f32[16,5120]{1,0:T(8,128)}, f32[16,16,5120]{2,1,0:T(8,128)S(1)}) fusion(f32[5120]{0:T(1024)S(1)} %copy-done.17, f32[16,16,5120]{2,1,0:T(8,128)} %get-tuple-element.12, f32[]{:T(128)} %bitcast.48, f32[]{:T(128)} %bitcast.33, f32[16,16,5120]{2,1,0:T(8,128)} %get-tuple-element.13, f32[16,16,5120]{2,1,0:T(8,128)} %copy-done.2, ...), kind=kLoop, calls=%fused_computation.21 | loop fusion | flops 32686080 | bytes 26624016 | tf_op jit(solution)/shard_map/reduce_sum | solution.py:89
  650.3 5.6 reshape.280
  660.5 5.7 copy.65
  666.2 7.0 reshape.281
  679.9 53.3 %all-gather.16.cloned.1.call-done = f32[128,5120]{1,0:T(8,128)} async-done(((f32[16,5120]{1,0:T(8,128)}), f32[128,5120]{1,0:T(8,128)}) %all-gather.16.cloned.1.call-update) | async-done | bytes 2621456 | tf_op jit(solution)/shard_map/all_gather | solution.py:53
  735.1 14.2 %multiply_reduce_fusion = (f32[]{:T(128)}, f32[16,16,5120]{2,1,0:T(8,128)}) fusion(f32[16,16,5120]{2,1,0:T(8,128)} %get-tuple-element.13, f32[16,16,5120]{2,1,0:T(8,128)} %copy-done.3, f32[5120]{0:T(1024)S(1)} %copy-done.17, f32[16,16,5120]{2,1,0:T(8,128)} %get-tuple-element.12, f32[]{:T(128)} %bitcast.48, f32[]{:T(128)} %bitcast.33, ...), kind=kOutput, calls=%fused_computation.20 | convolution fusion | flops 4054056960 | bytes 27193356 | tf_op jit(solution)/shard_map/dot_general | solution.py:74
  750.6 39.2 %psum.79 = f32[3]{0:T(128)S(1)} all-reduce(f32[3]{0:T(128)S(1)} %pad_maximum_fusion.4), channel_id=1, replica_groups=mesh['scen'=8,'gen'=4] {'scen','gen'}, use_global_device_ids=true, to_apply=%region_34.35 | all-reduce | flops 3 | bytes 24 | tf_op jit(solution)/shard_map/psum | solution.py:92
  791.9 10.7 %maximum_minimum_fusion = f32[16,16,5120]{2,1,0:T(8,128)} fusion(f32[16,16,5120]{2,1,0:T(8,128)} %copy-done.3, f32[16,16,5120]{2,1,0:T(8,128)} %get-tuple-element.59, f32[]{:T(128)} %bitcast.54, f32[]{:T(128)} %bitcast.44, f32[5120]{0:T(1024)S(1)} %copy-done.17, f32[5120]{0:T(1024)S(1)} %broadcast_add_fusion, f32[5120]{0:T(1024)S(1)} %get-tuple-element.25, ...), kind=kLoop, calls=%fused_computation.19 | loop fusion | flops 24903680 | bytes 26296336 | tf_op jit(solution)/shard_map/jit(clip)/min | solution.py:100
  (144 shorter events, 142.8 us)
Async XLA Ops:
  7.2 53.0 %copy-start = (bf16[20,256,256]{2,1,0:T(8,128)(2,1)S(1)}, bf16[20,256,256]{2,1,0:T(8,128)(2,1)}, u32[]{:S(2)}) copy-start(bf16[20,256,256]{2,1,0:T(8,128)(2,1)} %param.14) | copy-start | bytes 7864324
  7.2 2.5 copy-start.22
  7.2 79.3 %all-reduce.6.cloned.1.call-start = ((), (), s32[]{:S(2)}) async-start(), calls=%async_computation | async-start | bytes 524288 | tf_op jit(solution)/shard_map/psum | solution.py:61
  9.0 4.7 copy-start.17
  9.0 6.7 copy-start.27
  9.0 6.7 copy-start.25
  9.0 8.1 copy-start.26
  13.6 165.2 %all-reduce.8.cloned.1.call-start = ((), (), s32[]{:S(2)}) async-start(), calls=%async_computation.1 | async-start | bytes 524288 | tf_op jit(solution)/shard_map/psum | solution.py:61
  60.1 2.9 copy-start.5
  60.1 3.6 copy-start.11
  70.5 6.9 copy-start.24
  77.4 10.8 %copy-start.15 = (f32[16,16,256]{2,1,0:T(8,128)S(1)}, f32[16,16,256]{2,1,0:T(8,128)}, u32[]{:S(2)}) copy-start(f32[16,16,256]{2,1,0:T(8,128)} %param.10) | copy-start | bytes 786436
  146.0 89.5 %all-gather.10.cloned.1.call-start = ((), (), s32[]{:S(2)}) async-start(), calls=%async_computation.5 | async-start | bytes 2949120 | tf_op jit(solution)/shard_map/all_gather | solution.py:53
  146.7 193.6 %all-reduce.10.cloned.1.call-start = ((), (), s32[]{:S(2)}) async-start(), calls=%async_computation.2 | async-start | bytes 524288 | tf_op jit(solution)/shard_map/psum | solution.py:61
  158.7 2.9 copy-start.6
  158.7 3.7 copy-start.12
  307.6 89.8 %all-gather.12.cloned.1.call-start = ((), (), s32[]{:S(2)}) async-start(), calls=%async_computation.6 | async-start | bytes 2949120 | tf_op jit(solution)/shard_map/all_gather | solution.py:53
  308.2 202.1 %all-reduce.12.cloned.1.call-start = ((), (), s32[]{:S(2)}) async-start(), calls=%async_computation.3 | async-start | bytes 524288 | tf_op jit(solution)/shard_map/psum | solution.py:61
  320.5 2.9 copy-start.7
  320.5 3.7 copy-start.13
  330.9 10.5 %copy-start.18 = (f32[256,256]{1,0:T(8,128)S(1)}, f32[256,256]{1,0:T(8,128)}, u32[]{:S(2)}) copy-start(f32[256,256]{1,0:T(8,128)} %all-reduce.6.cloned.1.call-done) | copy-start | bytes 786436
  477.6 89.9 %all-gather.14.cloned.1.call-start = ((), (), s32[]{:S(2)}) async-start(), calls=%async_computation.7 | async-start | bytes 2949120 | tf_op jit(solution)/shard_map/all_gather | solution.py:53
  478.4 197.6 %all-reduce.14.cloned.1.call-start = ((), (), s32[]{:S(2)}) async-start(), calls=%async_computation.4 | async-start | bytes 524288 | tf_op jit(solution)/shard_map/psum | solution.py:61
  490.3 2.9 copy-start.8
  490.3 3.7 copy-start.14
  500.7 70.4 %copy-start.16 = (f32[256,256]{1,0:T(8,128)S(1)}, f32[256,256]{1,0:T(8,128)}, u32[]{:S(2)}) copy-start(f32[256,256]{1,0:T(8,128)} %all-reduce.10.cloned.1.call-done) | copy-start | bytes 786436
  643.2 89.9 %all-gather.16.cloned.1.call-start = ((), (), s32[]{:S(2)}) async-start(), calls=%async_computation.8 | async-start | bytes 2949120 | tf_op jit(solution)/shard_map/all_gather | solution.py:53
  655.9 2.9 copy-start.9
  655.9 3.7 copy-start.10
  735.1 14.2 %copy-start.23 = (f32[16,5120]{1,0:T(8,128)}, f32[16,5120]{1,0:T(8,128)S(1)}, u32[]{:S(2)}) copy-start(f32[16,5120]{1,0:T(8,128)S(1)} %broadcast_multiply_fusion) | copy-start | bytes 983044
  791.8 10.7 %copy-start.19 = (f32[256,256]{1,0:T(8,128)S(1)}, f32[256,256]{1,0:T(8,128)}, u32[]{:S(2)}) copy-start(f32[256,256]{1,0:T(8,128)} %all-reduce.14.cloned.1.call-done) | copy-start | bytes 786436
  791.8 10.7 %copy-start.21 = (f32[16,16,256]{2,1,0:T(8,128)S(1)}, f32[16,16,256]{2,1,0:T(8,128)}, u32[]{:S(2)}) copy-start(f32[16,16,256]{2,1,0:T(8,128)} %get-tuple-element.18) | copy-start | bytes 786436
  (5 other events, 9.9 us)
Sparse Core Ops, SparseCore 0:
  13.8 34.9 all-reduce.5
  146.1 32.6 all-reduce.7
  181.1 54.3 all-gather.9
  307.7 32.5 all-reduce.9
  342.9 54.3 all-gather.11
  477.7 32.5 all-reduce.11
  513.1 54.3 all-gather.13
  643.4 32.5 all-reduce.13
  678.7 54.3 all-gather.15
